TPU v7x, 32 devices: a whole 2x2x4 slice. The times are simulated.
32 devices in a mesh: site: 2 (over x), row: 4 (over z), col: 4 (over y, core).
Axes of the slice: x: 2, y: 2, z: 4, core: 2. Of those that a mesh axis runs over, the one named last changes fastest.
Arguments:
- pair_array: bfloat16 [128, 64, 128], P(('site', 'row'), 'col'), parts along dimension 0, may hold values from -6 to 6
- in_gain: float32 [128], replicated, may hold values from 0.25 to 1.75
- left_weight: bfloat16 [256, 128], P('site'), parts along dimension 0, may hold values from -0.5 to 0.5
- right_weight: bfloat16 [256, 128], P('site'), parts along dimension 0, may hold values from -0.5 to 0.5
- mid_gain: float32 [128], replicated, may hold values from 0.25 to 1.75
- out_weight: bfloat16 [256, 128], P('site'), parts along dimension 0, may hold values from -0.5 to 0.5
- out_gate: bfloat16 [256, 128], P('site'), parts along dimension 0, may hold values from -0.5 to 0.5
Outputs:
- triangle_out: bfloat16 [128, 64, 128], P(('site', 'row'), 'col'), parts along dimension 0
There are 2 independent parts, one for each index of `site`. A program takes and returns all parts, laid end to end along the dimension named above; an argument that names none is the same for every part. Nothing has to cross between parts.
All inputs are finite; a program needn't handle non-finite values.
Results may differ from a plain program's by a relative error of at most 0.012.
Values may be sent and summed in bfloat16 or wider, within the bound.
A program may use at most 64 MiB of HBM per device.

v0:
```python
import jax
import jax.numpy as jnp
from jax import lax
from jax.sharding import PartitionSpec as P


def norm_channels(values, channel_gain):
    centred = values - jnp.mean(values, axis=-1, keepdims=True)
    return (
        centred
        * lax.rsqrt(jnp.mean(centred * centred, axis=-1, keepdims=True) + 1e-05)
        * channel_gain
    )


def both_factors(pair_in, in_gain, left_weight, right_weight):
    ready = norm_channels(pair_in.astype(jnp.float32), in_gain).astype(jnp.bfloat16)
    ready = lax.optimization_barrier(ready)
    left = jnp.einsum("ijc,cd->ijd", ready, left_weight, preferred_element_type=jnp.float32)
    right = jnp.einsum("ijc,cd->ijd", ready, right_weight, preferred_element_type=jnp.float32)
    return (ready, left.astype(jnp.bfloat16), right.astype(jnp.bfloat16))


def finish_pair(mixed, ready, mid_gain, out_weight, out_gate):
    scaled = norm_channels(mixed.astype(jnp.float32), mid_gain).astype(jnp.bfloat16)
    scaled = lax.optimization_barrier(scaled)
    gate = jax.nn.sigmoid(
        jnp.einsum("ijc,cd->ijd", ready, out_gate, preferred_element_type=jnp.float32)
    )
    return (
        jnp.einsum("ijd,dc->ijc", scaled, out_weight, preferred_element_type=jnp.float32) * gate
    ).astype(jnp.bfloat16)


def body(pair_array, in_gain, left_weight, right_weight, mid_gain, out_weight, out_gate):
    ready, left, right = both_factors(pair_array, in_gain, left_weight, right_weight)
    count = pair_array.shape[0] * lax.axis_size("row")
    left_lines, right_lines = (
        lax.all_to_all(left, "row", split_axis=2, concat_axis=0, tiled=True),
        lax.all_to_all(right, "row", split_axis=2, concat_axis=0, tiled=True),
    )
    strip = jnp.einsum(
        "kid,kjd->ijd",
        lax.all_gather(left_lines, "col", axis=1, tiled=True),
        right_lines,
        preferred_element_type=jnp.float32,
    )
    strip = (strip * count ** (-0.5)).astype(jnp.bfloat16)
    mixed = lax.all_to_all(strip, "row", split_axis=0, concat_axis=2, tiled=True)
    return finish_pair(mixed, ready, mid_gain, out_weight, out_gate)


def solution(mesh):
    return jax.shard_map(
        body,
        mesh=mesh,
        in_specs=(
            P(("site", "row"), "col", None),
            P(),
            P("site", None),
            P("site", None),
            P(),
            P("site", None),
            P("site", None),
        ),
        out_specs=P(("site", "row"), "col", None),
        check_vma=False,
    )
```

profile of v0, /device:TPU:0, one launch (start us, length us, event | category | flops | bytes accessed | tf_op | source)
XLA Modules:
  0.0 46.4 jit_solution(6474242782185736790)
XLA Ops:
  0.0 0.0 copy-start
  0.0 0.0 copy-start.1
  0.0 1.0 %convert_reduce_fusion = f32[16,16]{1,0:T(8,128)S(1)} fusion(bf16[16,16,128]{2,1,0:T(8,128)(2,1)} %param.7), kind=kLoop, calls=%fused_computation.15 | loop fusion | flops 65280 | bytes 66560 | tf_op jit(solution)/shard_map/reduce_sum | solution.py:8
  1.0 0.0 copy-done.1
  1.0 0.2 fusion.10
  1.2 0.0 copy-start.4
  1.3 0.6 %copy-done.4 = f32[128]{0:T(128)S(1)} copy-done((f32[128]{0:T(128)S(1)}, f32[128]{0:T(128)}, u32[]{:S(2)}) %copy-start.4) | copy-done | bytes 536
  1.9 0.1 fusion.12
  2.0 0.0 copy-done
  2.0 0.1 convolution_convert_fusion.1
  2.2 0.4 copy.32
  2.6 1.2 %reshape.39 = bf16[4,2,4096]{2,1,0:T(2,128)(2,1)} reshape(bf16[128,16,16]{2,1,0:T(8,128)(2,1)S(1)} %bitcast.43) | data formatting | bytes 131072
  3.8 0.0 copy-start.2
  3.8 6.5 %all-to-all-start = ((bf16[4,2,4096]{2,1,0:T(2,128)(2,1)}), bf16[4,2,4096]{2,1,0:T(2,128)(2,1)S(1)}, u32[]{:S(2)}, u32[]{:S(2)}) async-start(bf16[4,2,4096]{2,1,0:T(2,128)(2,1)} %reshape.39), calls=%async_computation | async-start | bytes 131072 | tf_op jit(solution)/shard_map/all_to_all | solution.py:40
  10.3 0.0 copy-done.2
  10.3 0.1 convolution_convert_fusion
  10.4 0.4 copy.34
  10.9 1.2 %reshape.41 = bf16[4,2,4096]{2,1,0:T(2,128)(2,1)} reshape(bf16[128,16,16]{2,1,0:T(8,128)(2,1)S(1)} %bitcast.44) | data formatting | bytes 131072
  12.0 4.0 %all-to-all-done = bf16[4,2,4096]{2,1,0:T(2,128)(2,1)S(1)} async-done(((bf16[4,2,4096]{2,1,0:T(2,128)(2,1)}), bf16[4,2,4096]{2,1,0:T(2,128)(2,1)S(1)}, u32[]{:S(2)}, u32[]{:S(2)}) %all-to-all-start) | async-done | bytes 65568 | tf_op jit(solution)/shard_map/all_to_all | solution.py:40
  16.0 3.3 %all-to-all-start.1 = ((bf16[4,2,4096]{2,1,0:T(2,128)(2,1)}), bf16[4,2,4096]{2,1,0:T(2,128)(2,1)S(1)}, u32[]{:S(2)}, u32[]{:S(2)}) async-start(bf16[4,2,4096]{2,1,0:T(2,128)(2,1)} %reshape.41), calls=%async_computation.1 | async-start | bytes 131072 | tf_op jit(solution)/shard_map/all_to_all | solution.py:39
  19.3 0.4 reshape.40
  19.7 0.4 copy.33
  20.2 0.3 copy.37
  20.5 4.6 %all-to-all-done.1 = bf16[4,2,4096]{2,1,0:T(2,128)(2,1)S(1)} async-done(((bf16[4,2,4096]{2,1,0:T(2,128)(2,1)}), bf16[4,2,4096]{2,1,0:T(2,128)(2,1)S(1)}, u32[]{:S(2)}, u32[]{:S(2)}) %all-to-all-start.1) | async-done | bytes 65568 | tf_op jit(solution)/shard_map/all_to_all | solution.py:39
  25.0 0.4 reshape.42
  25.4 0.4 copy.35
  25.9 0.3 copy.36
  26.2 7.2 %all_gather.3 = bf16[64,64,32]{0,1,2:T(8,128)(2,1)S(1)} all-gather(bf16[64,16,32]{0,1,2:T(8,128)(2,1)S(1)} %copy.36), channel_id=1, replica_groups=mesh['site'=2,'row'=4,'col'=4] {'col'}, dimensions={1}, use_global_device_ids=true | all-gather | bytes 327680 | tf_op jit(solution)/shard_map/all_gather | solution.py:44
  33.4 0.4 fusion.1
  33.8 0.3 copy.38
  34.1 0.3 reshape.43
  34.4 8.1 %all_to_all.45 = bf16[4,2,4096]{2,1,0:T(2,128)(2,1)S(1)} all-to-all(bf16[4,2,4096]{2,1,0:T(2,128)(2,1)S(1)} %reshape.43), channel_id=1, replica_groups=mesh['site'=2,'row'=4,'col'=4] {'row'}, dimensions={0} | all-to-all | bytes 131072 | tf_op jit(solution)/shard_map/all_to_all | solution.py:49
  42.5 0.2 reshape.44
  42.7 0.1 fusion.7
  42.8 0.2 multiply_reduce_fusion
  43.1 0.3 copy.39
  43.4 0.0 copy-start.5
  43.5 0.3 reshape.32
  43.7 0.4 copy-done.5
  44.1 0.0 copy-start.3
  44.1 0.1 multiply_convert_fusion
  44.2 0.6 %copy-done.3 = bf16[128,128]{1,0:T(8,128)(2,1)S(1)} copy-done((bf16[128,128]{1,0:T(8,128)(2,1)S(1)}, bf16[128,128]{1,0:T(8,128)(2,1)}, u32[]{:S(2)}) %copy-start.3) | copy-done | bytes 32792
  44.9 0.0 copy-start.6
  44.9 0.1 fusion.14
  45.0 0.6 %copy-done.6 = bf16[128,128]{1,0:T(8,128)(2,1)S(1)} copy-done((bf16[128,128]{1,0:T(8,128)(2,1)S(1)}, bf16[128,128]{1,0:T(8,128)(2,1)}, u32[]{:S(2)}) %copy-start.6) | copy-done | bytes 32792
  45.6 0.8 %fusion.6 = bf16[16,16,128]{2,1,0:T(8,128)(2,1)} fusion(f32[16,16,128]{2,1,0:T(8,128)S(1)} %fusion.14, bf16[16,16,128]{2,1,0:T(8,128)(2,1)S(1)} %fusion.12, bf16[128,128]{1,0:T(8,128)(2,1)S(1)} %copy-done.6), kind=kOutput, calls=%fused_computation.8 | convolution fusion | flops 8552448 | bytes 294912 | tf_op jit(solution)/shard_map/ijc,cd->ijd/dot_general | solution.py:28
  (5 shorter events, 0.1 us)
Async XLA Ops:
  0.0 2.0 %copy-start = (bf16[128,128]{1,0:T(8,128)(2,1)S(1)}, bf16[128,128]{1,0:T(8,128)(2,1)}, u32[]{:S(2)}) copy-start(bf16[128,128]{1,0:T(8,128)(2,1)} %param.10) | copy-start | bytes 98308
  0.0 1.0 %copy-start.1 = (bf16[16,16,128]{2,1,0:T(8,128)(2,1)S(1)}, bf16[16,16,128]{2,1,0:T(8,128)(2,1)}, u32[]{:S(2)}) copy-start(bf16[16,16,128]{2,1,0:T(8,128)(2,1)} %param.7) | copy-start | bytes 196612
  1.2 0.7 %copy-start.4 = (f32[128]{0:T(128)S(1)}, f32[128]{0:T(128)}, u32[]{:S(2)}) copy-start(f32[128]{0:T(128)} %param.8) | copy-start | bytes 1540
  3.8 6.5 %copy-start.2 = (bf16[128,128]{1,0:T(8,128)(2,1)S(1)}, bf16[128,128]{1,0:T(8,128)(2,1)}, u32[]{:S(2)}) copy-start(bf16[128,128]{1,0:T(8,128)(2,1)} %param.9) | copy-start | bytes 98308
  3.8 12.2 %all-to-all-start = ((bf16[4,2,4096]{2,1,0:T(2,128)(2,1)}), bf16[4,2,4096]{2,1,0:T(2,128)(2,1)S(1)}, u32[]{:S(2)}, u32[]{:S(2)}) async-start(bf16[4,2,4096]{2,1,0:T(2,128)(2,1)} %reshape.39), calls=%async_computation | async-start | bytes 131072 | tf_op jit(solution)/shard_map/all_to_all | solution.py:40
  16.0 9.0 %all-to-all-start.1 = ((bf16[4,2,4096]{2,1,0:T(2,128)(2,1)}), bf16[4,2,4096]{2,1,0:T(2,128)(2,1)S(1)}, u32[]{:S(2)}, u32[]{:S(2)}) async-start(bf16[4,2,4096]{2,1,0:T(2,128)(2,1)} %reshape.41), calls=%async_computation.1 | async-start | bytes 131072 | tf_op jit(solution)/shard_map/all_to_all | solution.py:39
  43.4 0.7 %copy-start.5 = (f32[128]{0:T(128)S(1)}, f32[128]{0:T(128)}, u32[]{:S(2)}) copy-start(f32[128]{0:T(128)} %param.11) | copy-start | bytes 1540
  44.1 0.8 %copy-start.3 = (bf16[128,128]{1,0:T(8,128)(2,1)S(1)}, bf16[128,128]{1,0:T(8,128)(2,1)}, u32[]{:S(2)}) copy-start(bf16[128,128]{1,0:T(8,128)(2,1)} %param.12) | copy-start | bytes 98308
  44.9 0.8 %copy-start.6 = (bf16[128,128]{1,0:T(8,128)(2,1)S(1)}, bf16[128,128]{1,0:T(8,128)(2,1)}, u32[]{:S(2)}) copy-start(bf16[128,128]{1,0:T(8,128)(2,1)} %param.13) | copy-start | bytes 98308
where the time goes:
time: 47 us; the launch traced here: 46.4 us
  blocking collectives  15.3 us (33%)
  starting transfers between devices  9.76 us (21%)
  local copies, waits for them, and re-layouts  9.11 us (19%)
  waiting for transfers between devices  8.55 us (18%)
  other arithmetic  1.87 us (4%)
  matrix products  1.61 us (3%)
    all_to_all x1, blocking collectives, body(): lax.all_to_all(strip, 'row', split_axis=0, concat_axis=2, tiled=True)  8.11 us
    all_gather x1, blocking collectives, body(): lax.all_gather(left_lines, 'col', axis=1, tiled=True)  7.2 us
    all_to_all x1, starting transfers between devices, body(): lax.all_to_all(right, 'row', split_axis=2, concat_axis=0, tiled=True)  6.48 us
    unnamed x20, local copies, waits for them, and re-layouts  5.82 us
    all_to_all x1, waiting for transfers between devices, body(): lax.all_to_all(left, 'row', split_axis=2, concat_axis=0, tiled=True)  4.56 us
    all_to_all x1, waiting for transfers between devices, body(): lax.all_to_all(right, 'row', split_axis=2, concat_axis=0, tiled=True)  3.99 us
    all_to_all x1, starting transfers between devices, body(): lax.all_to_all(left, 'row', split_axis=2, concat_axis=0, tiled=True)  3.28 us
    reduce_sum x2, other arithmetic, norm_channels(): centred = values - jnp.mean(values, axis=-1, keepdims=True)  1.14 us
  transfers between devices with their start and end apart: 2, of which 2 were waited for; matrix products, arithmetic and copies ran while one was open for 6% of the time, Pallas kernels for 0%

commit v1 on v0

--- a/solution.py
+++ b/solution.py
@@ -2,6 +2,21 @@
 import jax.numpy as jnp
 from jax import lax
 from jax.sharding import PartitionSpec as P
+
+
+def work_around(array, axis, dim, make, out_dim):
+    ways, here, lap = (lax.axis_size(axis), lax.axis_index(axis), array.shape[dim])
+    results = []
+    for far in range(ways):
+        arriving = (
+            lax.ppermute(array, axis, [(d, (d + 1) % ways) for d in range(ways)])
+            if far + 1 < ways
+            else array
+        )
+        results.append(make(array, (here - far) % ways * lap))
+        array = arriving
+    line = jnp.concatenate(results[::-1], axis=out_dim)
+    return jnp.roll(line, (here + 1) * results[0].shape[out_dim], axis=out_dim)
 
 
 def norm_channels(values, channel_gain):
@@ -39,11 +54,14 @@
         lax.all_to_all(left, "row", split_axis=2, concat_axis=0, tiled=True),
         lax.all_to_all(right, "row", split_axis=2, concat_axis=0, tiled=True),
     )
-    strip = jnp.einsum(
-        "kid,kjd->ijd",
-        lax.all_gather(left_lines, "col", axis=1, tiled=True),
-        right_lines,
-        preferred_element_type=jnp.float32,
+    strip = work_around(
+        left_lines,
+        "col",
+        1,
+        lambda shard, at: jnp.einsum(
+            "kid,kjd->ijd", shard, right_lines, preferred_element_type=jnp.float32
+        ),
+        0,
     )
     strip = (strip * count ** (-0.5)).astype(jnp.bfloat16)
     mixed = lax.all_to_all(strip, "row", split_axis=0, concat_axis=2, tiled=True)

time: 47 us -> 54 us (1.15)
  waiting for transfers between devices: 8.55 us -> 21.2 us
  blocking collectives: 15.3 us -> 8.11 us
  local copies, waits for them, and re-layouts: 9.11 us -> 10.2 us
    ppermute x0 -> x3, waiting for transfers between devices: none -> 12.6 us  [work_around(): lax.ppermute(array, axis, [(d, (d + 1) % ways) for d in range(ways)])]
    all_gather x1 -> x0, blocking collectives: 7.2 us -> none  [body(): lax.all_gather(left_lines, 'col', axis=1, tiled=True)]
    concatenate x0 -> x1, local copies, waits for them, and re-layouts: none -> 0.82 us  [work_around(): return jnp.roll(line, (here + 1) * results[0].shape[out_dim], axis=out_dim)]
  transfers between devices with their start and end apart: 2 -> 5, of which waited for: 2 -> 5; matrix products, arithmetic and copies ran while one was open for 6% -> 6% of each run, Pallas kernels for 0% -> 0%
where the time goes in v1:
time: 54 us; the launch traced here: 53.5 us
  waiting for transfers between devices  21.2 us (39%)
  local copies, waits for them, and re-layouts  10.2 us (19%)
  starting transfers between devices  9.82 us (18%)
  blocking collectives  8.11 us (15%)
  other arithmetic  2.01 us (4%)
  matrix products  1.92 us (4%)
    ppermute x3, waiting for transfers between devices, work_around(): lax.ppermute(array, axis, [(d, (d + 1) % ways) for d in range(ways)])  12.6 us
    all_to_all x1, blocking collectives, body(): lax.all_to_all(strip, 'row', split_axis=0, concat_axis=2, tiled=True)  8.11 us
    all_to_all x1, starting transfers between devices, body(): lax.all_to_all(right, 'row', split_axis=2, concat_axis=0, tiled=True)  6.48 us
    unnamed x20, local copies, waits for them, and re-layouts  6.06 us
    all_to_all x1, waiting for transfers between devices, body(): lax.all_to_all(left, 'row', split_axis=2, concat_axis=0, tiled=True)  4.54 us
    all_to_all x1, waiting for transfers between devices, body(): lax.all_to_all(right, 'row', split_axis=2, concat_axis=0, tiled=True)  4 us
    all_to_all x1, starting transfers between devices, body(): lax.all_to_all(left, 'row', split_axis=2, concat_axis=0, tiled=True)  3.28 us
    reduce_sum x2, other arithmetic, norm_channels(): centred = values - jnp.mean(values, axis=-1, keepdims=True)  1.14 us
  transfers between devices with their start and end apart: 5, of which 5 were waited for; matrix products, arithmetic and copies ran while one was open for 6% of the time, Pallas kernels for 0%

profile of v1, /device:TPU:0, one launch (start us, length us, event | category | flops | bytes accessed | tf_op | source)
XLA Modules:
  0.0 53.5 jit_solution(14726265388144336870)
XLA Ops:
  0.0 1.0 %convert_reduce_fusion = f32[16,16]{1,0:T(8,128)S(1)} fusion(bf16[16,16,128]{2,1,0:T(8,128)(2,1)} %param.7), kind=kLoop, calls=%fused_computation.17 | loop fusion | flops 65280 | bytes 66560 | tf_op jit(solution)/shard_map/reduce_sum | solution.py:23
  1.0 0.2 fusion.8
  1.2 0.0 copy-start.4
  1.3 0.6 %copy-done.4 = f32[128]{0:T(128)S(1)} copy-done((f32[128]{0:T(128)S(1)}, f32[128]{0:T(128)}, u32[]{:S(2)}) %copy-start.4) | copy-done | bytes 536
  1.9 0.1 fusion.10
  2.0 0.1 convolution_convert_fusion.1
  2.2 0.4 copy.44
  2.6 1.2 %reshape.39 = bf16[4,2,4096]{2,1,0:T(2,128)(2,1)} reshape(bf16[128,16,16]{2,1,0:T(8,128)(2,1)S(1)} %bitcast.55) | data formatting | bytes 131072
  3.8 6.5 %all-to-all-start = ((bf16[4,2,4096]{2,1,0:T(2,128)(2,1)}), bf16[4,2,4096]{2,1,0:T(2,128)(2,1)S(1)}, u32[]{:S(2)}, u32[]{:S(2)}) async-start(bf16[4,2,4096]{2,1,0:T(2,128)(2,1)} %reshape.39), calls=%async_computation | async-start | bytes 131072 | tf_op jit(solution)/shard_map/all_to_all | solution.py:55
  10.3 0.1 convolution_convert_fusion
  10.4 0.4 copy.46
  10.9 1.2 %reshape.41 = bf16[4,2,4096]{2,1,0:T(2,128)(2,1)} reshape(bf16[128,16,16]{2,1,0:T(8,128)(2,1)S(1)} %bitcast.56) | data formatting | bytes 131072
  12.0 4.0 %all-to-all-done = bf16[4,2,4096]{2,1,0:T(2,128)(2,1)S(1)} async-done(((bf16[4,2,4096]{2,1,0:T(2,128)(2,1)}), bf16[4,2,4096]{2,1,0:T(2,128)(2,1)S(1)}, u32[]{:S(2)}, u32[]{:S(2)}) %all-to-all-start) | async-done | bytes 65568 | tf_op jit(solution)/shard_map/all_to_all | solution.py:55
  16.0 3.3 %all-to-all-start.1 = ((bf16[4,2,4096]{2,1,0:T(2,128)(2,1)}), bf16[4,2,4096]{2,1,0:T(2,128)(2,1)S(1)}, u32[]{:S(2)}, u32[]{:S(2)}) async-start(bf16[4,2,4096]{2,1,0:T(2,128)(2,1)} %reshape.41), calls=%async_computation.1 | async-start | bytes 131072 | tf_op jit(solution)/shard_map/all_to_all | solution.py:54
  19.3 0.4 reshape.40
  19.7 0.4 copy.45
  20.2 0.3 copy.49
  20.5 4.5 %all-to-all-done.1 = bf16[4,2,4096]{2,1,0:T(2,128)(2,1)S(1)} async-done(((bf16[4,2,4096]{2,1,0:T(2,128)(2,1)}), bf16[4,2,4096]{2,1,0:T(2,128)(2,1)S(1)}, u32[]{:S(2)}, u32[]{:S(2)}) %all-to-all-start.1) | async-done | bytes 65568 | tf_op jit(solution)/shard_map/all_to_all | solution.py:54
  25.0 0.4 reshape.42
  25.4 0.4 copy.47
  25.9 0.3 copy.48
  26.2 0.1 collective-permute-start
  26.3 0.2 convolution_bitcast_fusion
  26.4 4.2 %collective-permute-done = bf16[64,16,32]{0,1,2:T(8,128)(2,1)S(1)} collective-permute-done((bf16[64,16,32]{0,1,2:T(8,128)(2,1)S(1)}, bf16[64,16,32]{0,1,2:T(8,128)(2,1)S(1)}, u32[]{:S(2)}, u32[]{:S(2)}) %collective-permute-start) | collective-permute-done | bytes 65568 | tf_op jit(solution)/shard_map/ppermute | solution.py:12
  30.6 0.0 collective-permute-start.1
  30.6 0.2 convolution_bitcast_fusion.1
  30.8 4.2 %collective-permute-done.1 = bf16[64,16,32]{0,1,2:T(8,128)(2,1)S(1)} collective-permute-done((bf16[64,16,32]{0,1,2:T(8,128)(2,1)S(1)}, bf16[64,16,32]{0,1,2:T(8,128)(2,1)S(1)}, u32[]{:S(2)}, u32[]{:S(2)}) %collective-permute-start.1) | collective-permute-done | bytes 65568 | tf_op jit(solution)/shard_map/ppermute | solution.py:12
  35.0 0.0 collective-permute-start.2
  35.0 0.2 convolution_bitcast_fusion.2
  35.2 4.2 %collective-permute-done.2 = bf16[64,16,32]{0,1,2:T(8,128)(2,1)S(1)} collective-permute-done((bf16[64,16,32]{0,1,2:T(8,128)(2,1)S(1)}, bf16[64,16,32]{0,1,2:T(8,128)(2,1)S(1)}, u32[]{:S(2)}, u32[]{:S(2)}) %collective-permute-start.2) | collective-permute-done | bytes 65568 | tf_op jit(solution)/shard_map/ppermute | solution.py:12
  39.4 0.2 convolution_bitcast_fusion.3
  39.6 0.8 %concatenate.6 = f32[128,16,32]{0,1,2:T(8,128)S(1)} concatenate(f32[16,16,32]{0,1,2:T(8,128)S(1)} %convolution_bitcast_fusion.3, f32[16,16,32]{0,1,2:T(8,128)S(1)} %convolution_bitcast_fusion.2, f32[16,16,32]{0,1,2:T(8,128)S(1)} %convolution_bitcast_fusion.1, f32[16,16,32]{0,1,2:T(8,128)S(1)} %convolution_bitcast_fusion, f32[16,16,32]{0,1,2:T(8,128)S(1)} %convolution_bitcast_fusion.3, ...), dimensions={0} | concatenate | bytes 524288 | tf_op jit(solution)/shard_map/jit(_roll_dynamic)/concatenate | solution.py:19
  40.4 0.1 multiply_convert_fusion
  40.6 0.3 copy.54
  40.9 0.3 reshape.43
  41.2 8.1 %all_to_all.45 = bf16[4,2,4096]{2,1,0:T(2,128)(2,1)S(1)} all-to-all(bf16[4,2,4096]{2,1,0:T(2,128)(2,1)S(1)} %reshape.43), channel_id=1, replica_groups=mesh['site'=2,'row'=4,'col'=4] {'row'}, dimensions={0} | all-to-all | bytes 131072 | tf_op jit(solution)/shard_map/all_to_all | solution.py:67
  49.3 0.2 reshape.44
  49.5 0.3 copy.55
  49.8 0.3 reshape.32
  50.1 0.1 fusion.5
  50.2 0.2 multiply_reduce_fusion
  50.5 0.0 copy-start.5
  50.5 0.6 %copy-done.5 = f32[128]{0:T(128)S(1)} copy-done((f32[128]{0:T(128)S(1)}, f32[128]{0:T(128)}, u32[]{:S(2)}) %copy-start.5) | copy-done | bytes 536
  51.1 0.1 multiply_convert_fusion.1
  51.3 0.6 %copy-done.3 = bf16[128,128]{1,0:T(8,128)(2,1)S(1)} copy-done((bf16[128,128]{1,0:T(8,128)(2,1)S(1)}, bf16[128,128]{1,0:T(8,128)(2,1)}, u32[]{:S(2)}) %copy-start.3) | copy-done | bytes 32792
  51.9 0.1 fusion.12
  52.0 0.6 %copy-done.6 = bf16[128,128]{1,0:T(8,128)(2,1)S(1)} copy-done((bf16[128,128]{1,0:T(8,128)(2,1)S(1)}, bf16[128,128]{1,0:T(8,128)(2,1)}, u32[]{:S(2)}) %copy-start.6) | copy-done | bytes 32792
  52.6 0.8 %fusion.4 = bf16[16,16,128]{2,1,0:T(8,128)(2,1)} fusion(f32[16,16,128]{2,1,0:T(8,128)S(1)} %fusion.12, bf16[16,16,128]{2,1,0:T(8,128)(2,1)S(1)} %fusion.10, bf16[128,128]{1,0:T(8,128)(2,1)S(1)} %copy-done.6), kind=kOutput, calls=%fused_computation.9 | convolution fusion | flops 8552448 | bytes 294912 | tf_op jit(solution)/shard_map/ijc,cd->ijd/dot_general | solution.py:43
  (13 shorter events, 0.1 us)
Async XLA Ops:
  0.0 2.0 %copy-start = (bf16[128,128]{1,0:T(8,128)(2,1)S(1)}, bf16[128,128]{1,0:T(8,128)(2,1)}, u32[]{:S(2)}) copy-start(bf16[128,128]{1,0:T(8,128)(2,1)} %param.10) | copy-start | bytes 98308
  0.0 1.0 %copy-start.1 = (bf16[16,16,128]{2,1,0:T(8,128)(2,1)S(1)}, bf16[16,16,128]{2,1,0:T(8,128)(2,1)}, u32[]{:S(2)}) copy-start(bf16[16,16,128]{2,1,0:T(8,128)(2,1)} %param.7) | copy-start | bytes 196612
  1.2 0.7 %copy-start.4 = (f32[128]{0:T(128)S(1)}, f32[128]{0:T(128)}, u32[]{:S(2)}) copy-start(f32[128]{0:T(128)} %param.8) | copy-start | bytes 1540
  3.8 6.5 %copy-start.2 = (bf16[128,128]{1,0:T(8,128)(2,1)S(1)}, bf16[128,128]{1,0:T(8,128)(2,1)}, u32[]{:S(2)}) copy-start(bf16[128,128]{1,0:T(8,128)(2,1)} %param.9) | copy-start | bytes 98308
  3.8 12.2 %all-to-all-start = ((bf16[4,2,4096]{2,1,0:T(2,128)(2,1)}), bf16[4,2,4096]{2,1,0:T(2,128)(2,1)S(1)}, u32[]{:S(2)}, u32[]{:S(2)}) async-start(bf16[4,2,4096]{2,1,0:T(2,128)(2,1)} %reshape.39), calls=%async_computation | async-start | bytes 131072 | tf_op jit(solution)/shard_map/all_to_all | solution.py:55
  16.0 9.0 %all-to-all-start.1 = ((bf16[4,2,4096]{2,1,0:T(2,128)(2,1)}), bf16[4,2,4096]{2,1,0:T(2,128)(2,1)S(1)}, u32[]{:S(2)}, u32[]{:S(2)}) async-start(bf16[4,2,4096]{2,1,0:T(2,128)(2,1)} %reshape.41), calls=%async_computation.1 | async-start | bytes 131072 | tf_op jit(solution)/shard_map/all_to_all | solution.py:54
  26.2 4.4 %collective-permute-start = (bf16[64,16,32]{0,1,2:T(8,128)(2,1)S(1)}, bf16[64,16,32]{0,1,2:T(8,128)(2,1)S(1)}, u32[]{:S(2)}, u32[]{:S(2)}) collective-permute-start(bf16[64,16,32]{0,1,2:T(8,128)(2,1)S(1)} %copy.48), channel_id=1, source_target_pairs={{0,1},{1,2},{2,3},{3,0},{4,5},{5,6},{6,7},{7,4},{8,9},{9,10},{10,1... | collective-permute-start | bytes 196616 | tf_op jit(solution)/shard_map/ppermute | solution.py:12
  30.6 4.4 %collective-permute-start.1 = (bf16[64,16,32]{0,1,2:T(8,128)(2,1)S(1)}, bf16[64,16,32]{0,1,2:T(8,128)(2,1)S(1)}, u32[]{:S(2)}, u32[]{:S(2)}) collective-permute-start(bf16[64,16,32]{0,1,2:T(8,128)(2,1)S(1)} %collective-permute-done), channel_id=1, source_target_pairs={{0,1},{1,2},{2,3},{3,0},{4,5},{5,6},{6,7},{7,4},{8,9},{9,10},{10,1... | collective-permute-start | bytes 196616 | tf_op jit(solution)/shard_map/ppermute | solution.py:12
  35.0 4.4 %collective-permute-start.2 = (bf16[64,16,32]{0,1,2:T(8,128)(2,1)S(1)}, bf16[64,16,32]{0,1,2:T(8,128)(2,1)S(1)}, u32[]{:S(2)}, u32[]{:S(2)}) collective-permute-start(bf16[64,16,32]{0,1,2:T(8,128)(2,1)S(1)} %collective-permute-done.1), channel_id=1, source_target_pairs={{0,1},{1,2},{2,3},{3,0},{4,5},{5,6},{6,7},{7,4},{8,9},{9,10},{10,1... | collective-permute-start | bytes 196616 | tf_op jit(solution)/shard_map/ppermute | solution.py:12
  50.5 0.7 %copy-start.5 = (f32[128]{0:T(128)S(1)}, f32[128]{0:T(128)}, u32[]{:S(2)}) copy-start(f32[128]{0:T(128)} %param.11) | copy-start | bytes 1540
  51.1 0.8 %copy-start.3 = (bf16[128,128]{1,0:T(8,128)(2,1)S(1)}, bf16[128,128]{1,0:T(8,128)(2,1)}, u32[]{:S(2)}) copy-start(bf16[128,128]{1,0:T(8,128)(2,1)} %param.12) | copy-start | bytes 98308
  51.9 0.8 %copy-start.6 = (bf16[128,128]{1,0:T(8,128)(2,1)S(1)}, bf16[128,128]{1,0:T(8,128)(2,1)}, u32[]{:S(2)}) copy-start(bf16[128,128]{1,0:T(8,128)(2,1)} %param.13) | copy-start | bytes 98308
